TPU v7x, 32 devices: a whole 2x2x4 slice. The times are simulated.
32 devices in a mesh: seq: 16 (over z, y, x), rep: 2 (over core).
Axes of the slice: x: 2, y: 2, z: 4, core: 2. Of those that a mesh axis runs over, the one named last changes fastest.
Arguments:
- queries: bfloat16 [4096, 4096], P(('rep', 'seq')), parts along dimension 0, may hold values from -160 to 160
- keys_values: bfloat16 [2, 4096, 1024], P(None, ('rep', 'seq')), parts along dimension 1, may hold values from -6 to 6
- segment_ids: int32 [4096], P(('rep', 'seq')), parts along dimension 0, may hold values from 0 to 31, never falling along the last dimension, each value on 1 to 1024 neighbouring positions
Outputs:
- attended: bfloat16 [4096, 4096], P(('rep', 'seq')), parts along dimension 0
There are 2 independent parts, one for each index of `rep`. A program takes and returns all parts, laid end to end along the dimension named above; each array names one. Nothing has to cross between parts.
Inputs may be any that keep to these rules, and one draw needn't show every extreme that they name: `segment_ids`: ids never fall along the tokens; every document holds 1 to 1024 consecutive tokens, one exactly 1024.
All inputs are finite; a program needn't handle non-finite values.
Results may differ from a plain program's by a relative error of at most 0.004.
Values may be sent and summed in bfloat16 or wider, within the bound.
A program may use at most 192 MiB of HBM per device.

v0:
```python
import functools
import math

import jax
import jax.numpy as jnp
from jax import lax
from jax.experimental import pallas as pl
from jax.experimental.pallas import tpu as pltpu
from jax.sharding import PartitionSpec as P

HQ = 32
HK = 8
DH = 128
WINDOW = 2048
GROUP = HQ // HK
SPAN = 4
CHUNKS = 8
RELAY_LAG, USE_LAG, LAST_LAG, TAIL_LAG = 4, 13, 6, 11
PER = HK // CHUNKS
NEG_BIG = -1e30
SCALE2 = DH ** (-0.5) * math.log2(math.e)


def kernel(n, rows, back, q_hbm, kv_hbm, ids_hbm, out_hbm, buf, ids_buf, q_buf, out_buf, bias, run_max, run_sum, run_acc,
           in_sem, out_sem, send_sem, recv_sem):
    last = back // SPAN
    planes = n // SPAN
    me = lax.axis_index("seq")
    plane = me // SPAN
    spot = me % SPAN
    low, high = spot % 2, spot // 2
    spot_x = (1 - low) + 2 * high
    spot_y = low + 2 * (1 - high)
    spot_d = (1 - low) + 2 * (1 - high)
    spots = (spot, spot_x, spot_y, spot_d)
    dev_x = plane * SPAN + spot_x
    dev_y = plane * SPAN + spot_y
    up_ok = plane < planes - 1
    down_ok = plane > 0
    dev_up = jnp.where(up_ok, me + SPAN, me - SPAN)
    dev_down = jnp.where(down_ok, me - SPAN, me + SPAN)
    ids_piece = CHUNKS

    def need(s, to, block):
        gap = SPAN * s + to - block
        return (plane >= s) & (gap >= 1) & (gap <= back)

    def via_x(s, block, c):
        mixed = (block % 2) != (block // 2)
        first = c < CHUNKS // 2 or c == ids_piece
        middle = 0 < s < last
        if first and middle:
            return block >= 0
        if first:
            return jnp.logical_not(mixed)
        if middle:
            return mixed
        return block < 0

    def ref_of(s, r, c):
        if c == ids_piece:
            return ids_buf.at[s, r]
        return buf.at[s, pl.ds(c * PER, PER), :, r]

    def copy(s, r, c, lane, to_s, to_r, device):
        return pltpu.make_async_remote_copy(
            src_ref=ref_of(s, r, c),
            dst_ref=ref_of(to_s, to_r, c),
            send_sem=send_sem.at[s, lane, c],
            recv_sem=recv_sem.at[to_s, to_r, c],
            device_id={"seq": device},
            device_id_type=pl.DeviceIdType.MESH,
        )

    def forwards(s, c):
        out = [
            (need(s, spot_x, spot), copy(s, 0, c, 0, s, 1, dev_x)),
            (need(s, spot_y, spot), copy(s, 0, c, 1, s, 2, dev_y)),
        ]
        if s < last:
            out.insert(0, (up_ok & (plane >= s), copy(s, 0, c, 2, s + 1, 0, dev_up)))
        return out

    def relay_x(s, c):
        return (need(s, spot_y, spot_x) & via_x(s, spot_x, c), copy(s, 1, c, 3, s, 3, dev_y))

    def relay_y(s, c):
        return (need(s, spot_x, spot_y) & jnp.logical_not(via_x(s, spot_y, c)), copy(s, 2, c, 4, s, 3, dev_x))

    def start(pair):
        @pl.when(pair[0])
        def _():
            pair[1].start()

    def wait_in(s, r, c):
        cond = (plane >= s) if r == 0 else need(s, spot, spots[r])

        @pl.when(cond)
        def _():
            copy(s, r, c, 0, s, r, dev_x).wait_recv()

    kv_in = [
        pltpu.make_async_copy(kv_hbm.at[:, :, pl.ds(h * DH, DH)], buf.at[0, h, :, 0], in_sem.at[h]) for h in range(HK)
    ]
    ids_in = pltpu.make_async_copy(ids_hbm, ids_buf.at[0, 0], in_sem.at[HK])
    q_in = pltpu.make_async_copy(q_hbm, q_buf, in_sem.at[HK + 1])
    ids_in.start()
    for one in kv_in:
        one.start()
    q_in.start()

    barrier = pltpu.get_barrier_semaphore()
    for cond, device in ((None, dev_x), (None, dev_y), (up_ok, dev_up), (down_ok, dev_down)):
        def greet(device=device):
            pl.semaphore_signal(barrier, inc=1, device_id={"seq": device}, device_id_type=pl.DeviceIdType.MESH)
        if cond is None:
            greet()
        else:
            pl.when(cond)(greet)
    pl.semaphore_wait(barrier, 2 + up_ok.astype(jnp.int32) + down_ok.astype(jnp.int32))

    pieces = [ids_piece] + list(range(CHUNKS))
    for c in pieces:
        if c == ids_piece:
            ids_in.wait()
        else:
            for h in range(c * PER, (c + 1) * PER):
                kv_in[h].wait()
        for pair in forwards(0, c):
            start(pair)

    for s in range(last + 1):
        for r in range(SPAN):
            if s == 0 and r == 0:
                continue
            absent = (plane < s) if r == 0 else jnp.logical_not(need(s, spot, spots[r]))

            @pl.when(absent)
            def _():
                ids_buf[s, r] = jnp.zeros((1, rows), jnp.int32)

                def clear(h, carry):
                    for k in range(2):
                        buf[s, h, k, r] = jnp.zeros((rows, DH), buf.dtype)
                    return carry

                lax.fori_loop(0, HK, clear, 0)

    q_in.wait()

    def make_bias(s, begin, end):
        own = jnp.broadcast_to(ids_buf[0, 0].astype(jnp.float32), (rows, rows)).T
        row = lax.broadcasted_iota(jnp.int32, (rows, rows), 0)
        col = lax.broadcasted_iota(jnp.int32, (rows, rows), 1)
        for r in range(begin, end):
            gap = SPAN * s + spot - spots[r]
            limit = jnp.where((plane >= s) & (gap <= back), WINDOW, 0)
            distance = gap * rows + row - col
            other = jnp.broadcast_to(ids_buf[s, r].astype(jnp.float32), (rows, rows))
            allowed = (own == other) & (distance >= 0) & (distance < limit)
            bias[s, :, r * rows:(r + 1) * rows] = jnp.where(allowed, 0.0, NEG_BIG)

    def attend(s, h, begin, end):
        first, final = s == 0, s == last and end == SPAN
        span = (end - begin) * rows
        cols = pl.ds(pl.multiple_of(h * GROUP * DH, GROUP * DH), GROUP * DH)
        wide = q_buf[:, cols]
        q = jnp.concatenate([wide[:, g * DH:(g + 1) * DH] for g in range(GROUP)], axis=0)
        k = buf[s, h, 0, begin:end].reshape(span, DH)
        v = buf[s, h, 1, begin:end].reshape(span, DH)
        t = lax.dot_general(q, k, (((1,), (1,)), ((), ())), preferred_element_type=jnp.float32)
        t = (t * SCALE2).reshape(GROUP, rows, span) + bias[s, :, begin * rows:end * rows][None]
        t = t.reshape(GROUP * rows, span)
        top = jnp.max(t, axis=1, keepdims=True)
        if first:
            new = jnp.broadcast_to(top, (GROUP * rows, DH))
        else:
            old = run_max[h]
            new = jnp.maximum(old, top)
        p = [jnp.exp2(t[:, r * rows:(r + 1) * rows] - new) for r in range(end - begin)]
        total = functools.reduce(lambda x, y: x + y, p)
        w = jnp.concatenate([one.astype(jnp.bfloat16) for one in p], axis=1)
        acc = jnp.dot(w, v, preferred_element_type=jnp.float32)
        if not first:
            fix = jnp.exp2(old - new)
            total = total + run_sum[h] * fix
            acc = acc + run_acc[h] * fix
        if final:
            o = (acc / jnp.sum(total, axis=1, keepdims=True)).astype(out_buf.dtype)
            out_buf[:, cols] = jnp.concatenate([o[g * rows:(g + 1) * rows] for g in range(GROUP)], axis=1)
        else:
            run_max[h] = new
            run_sum[h] = total
            run_acc[h] = acc

    def out_copy(c):
        cols = pl.ds(c * PER * GROUP * DH, PER * GROUP * DH)
        return pltpu.make_async_copy(out_buf.at[:, cols], out_hbm.at[:, cols], out_sem.at[c])

    def consume(s, c, begin, end):
        if end == SPAN:
            wait_in(s, SPAN - 1, c)
        if c == ids_piece:
            make_bias(s, begin, end)
            return

        def body(h, carry):
            attend(s, h, begin, end)
            return carry

        lax.fori_loop(c * PER, (c + 1) * PER, body, 0)
        if s == last and end == SPAN:
            out_copy(c).start()

    def pass_on(s, c):
        wait_in(s, 0, c)
        for pair in forwards(s, c):
            start(pair)

    def relay(s, c):
        wait_in(s, 1, c)
        start(relay_x(s, c))
        wait_in(s, 2, c)
        start(relay_y(s, c))

    steps = []
    for s in range(last + 1):
        for place, c in enumerate(pieces):
            now = s * len(pieces) + place
            if s > 0:
                steps.append((now - len(pieces), 0, functools.partial(pass_on, s, c)))
            steps.append((now + (RELAY_LAG if 0 < s < last else 0), 1, functools.partial(relay, s, c)))
            if s < last:
                steps.append((now + USE_LAG, 2, functools.partial(consume, s, c, 0, SPAN)))
            else:
                steps.append((now + LAST_LAG, 3, functools.partial(consume, s, c, 0, SPAN - 1)))
                steps.append((now + TAIL_LAG, 4, functools.partial(consume, s, c, SPAN - 1, SPAN)))
    for _, _, step in sorted(steps, key=lambda one: one[:2]):
        step()

    for s in range(last + 1):
        for c in pieces:
            for cond, one in forwards(s, c) + [relay_x(s, c), relay_y(s, c)]:
                @pl.when(cond)
                def _():
                    one.wait_send()
    for c in range(CHUNKS):
        out_copy(c).wait()


def solution(mesh):
    n = mesh.shape["seq"]

    def local(queries, keys_values, segment_ids):
        rows = queries.shape[0]
        reach = min(WINDOW, n * rows // 2)
        back = -(-(reach - 1) // rows)
        assert n % SPAN == 0 and back % SPAN == 0
        sets = back // SPAN + 1
        group_rows = GROUP * rows
        return pl.pallas_call(
            functools.partial(kernel, n, rows, back),
            out_shape=jax.ShapeDtypeStruct(queries.shape, queries.dtype),
            in_specs=[pl.BlockSpec(memory_space=pl.ANY)] * 3,
            out_specs=pl.BlockSpec(memory_space=pl.ANY),
            scratch_shapes=[
                pltpu.VMEM((sets, HK, 2, SPAN, rows, DH), jnp.bfloat16),
                pltpu.VMEM((sets, SPAN, 1, rows), jnp.int32),
                pltpu.VMEM((rows, HQ * DH), jnp.bfloat16),
                pltpu.VMEM((rows, HQ * DH), jnp.bfloat16),
                pltpu.VMEM((sets, rows, SPAN * rows), jnp.float32),
                pltpu.VMEM((HK, group_rows, DH), jnp.float32),
                pltpu.VMEM((HK, group_rows, DH), jnp.float32),
                pltpu.VMEM((HK, group_rows, DH), jnp.float32),
                pltpu.SemaphoreType.DMA((HK + 2,)),
                pltpu.SemaphoreType.DMA((CHUNKS,)),
                pltpu.SemaphoreType.DMA((sets, 5, CHUNKS + 1)),
                pltpu.SemaphoreType.DMA((sets, SPAN, CHUNKS + 1)),
            ],
            compiler_params=pltpu.CompilerParams(
                collective_id=0, has_side_effects=True, vmem_limit_bytes=60 * 1024 * 1024
            ),
        )(queries, keys_values, segment_ids.reshape(1, rows))

    return jax.shard_map(
        local,
        mesh=mesh,
        in_specs=(P(("rep", "seq"), None), P(None, ("rep", "seq"), None), P(("rep", "seq"))),
        out_specs=P(("rep", "seq"), None),
        check_vma=False,
    )
```

profile of v0, /device:TPU:28, one launch (start us, length us, event | category | flops | bytes accessed | tf_op | source)
XLA Modules:
  0.0 53.8 jit_solution(529380570625093189)
XLA Ops:
  0.0 51.5 %shard_map.37 = bf16[128,4096]{1,0:T(8,128)(2,1)} custom-call(bf16[128,4096]{1,0:T(8,128)(2,1)} %q_hbm.1, bf16[2,128,1024]{2,1,0:T(8,128)(2,1)} %kv_hbm.1, s32[1,128]{1,0:T(1,128)} %bitcast.1), custom_call_target="tpu_custom_call" | custom-call | tf_op jit(solution)/shard_map/pallas_call | solution.py:261
  51.5 2.3 %copy.5 = bf16[128,4096]{1,0:T(8,128)(2,1)} copy(bf16[128,4096]{1,0:T(8,128)(2,1)} %shard_map.37) | data formatting | bytes 2097152
where the time goes:
time: 53.9 us; the launch traced here: 53.8 us
  Pallas kernels  51.5 us (96%)
  local copies, waits for them, and re-layouts  2.29 us (4%)
    pallas_call x1, Pallas kernels, local(): pl.pallas_call(functools.partial(kernel, n, rows, back), out_shape=jax.Sh...  51.5 us
    unnamed x1, local copies, waits for them, and re-layouts  2.29 us

commit v1 on v0

v1 whole, which is shorter than its diff:
```python
import functools
import math

import jax
import jax.numpy as jnp
from jax import lax
from jax.experimental import pallas as pl
from jax.experimental.pallas import tpu as pltpu
from jax.sharding import PartitionSpec as P

HQ = 32
HK = 8
DH = 128
WINDOW = 2048
GROUP = HQ // HK
WIDE = GROUP * DH
SPAN = 4
SERVED = 4
NEG_BIG = -1e30
SCALE2 = DH ** (-0.5) * math.log2(math.e)
IDS = HK
PIECES = [IDS] + list(range(HK))


def kernel(n, rows, back, q_hbm, kv_hbm, ids_hbm, out_hbm, buf, ids_buf, q_buf, q_up, ids_up, out_buf, part_out, part_in,
           lse_out, lse_in, bias, bias_up, run_max, run_sum, run_acc, in_sem, out_sem, send_sem, recv_sem, down_send,
           down_recv, part_send, part_recv):
    top_level = back // SPAN
    planes = n // SPAN
    group_rows = GROUP * rows
    me = lax.axis_index("seq")
    plane = me // SPAN
    spot = me % SPAN
    low, high = spot % 2, spot // 2
    spot_x = (1 - low) + 2 * high
    spot_y = low + 2 * (1 - high)
    spot_d = (1 - low) + 2 * (1 - high)
    spots = (spot, spot_x, spot_y, spot_d)
    dev_x = plane * SPAN + spot_x
    dev_y = plane * SPAN + spot_y
    up_ok = plane < planes - 1
    down_ok = plane > 0
    dev_up = jnp.where(up_ok, me + SPAN, me - SPAN)
    dev_down = jnp.where(down_ok, me - SPAN, me + SPAN)

    def last_of(c):
        return top_level - 1 if c < SERVED else top_level

    def later(block, t):
        return (block > t).astype(jnp.int32)

    def need(s, t, block, c):
        gap = SPAN * s + t - block
        return (plane >= s) & (gap >= 1) & (gap <= SPAN * last_of(c))

    def ends_in_x(s, t, c):
        mixed = (t % 2) != (t // 2)
        edge = s == 0 or s == last_of(c)
        if edge:
            return mixed | (c % 2 == 0)
        return jnp.logical_not(mixed) & (c % 2 == 0)

    def ref_of(level, r, c):
        if c == IDS:
            return ids_buf.at[level, r]
        return buf.at[level, c, :, r]

    def copy(s, r, c, lane, to_s, to_r, device, to_spot):
        level, to_level = s - later(spots[r], spot), to_s - later(spots[r], to_spot)
        return pltpu.make_async_remote_copy(
            src_ref=ref_of(level, r, c),
            dst_ref=ref_of(to_level, to_r, c),
            send_sem=send_sem.at[s, lane, c],
            recv_sem=recv_sem.at[to_level, to_r, c],
            device_id={"seq": device},
            device_id_type=pl.DeviceIdType.MESH,
        )

    def wait_slot(level, r, c):
        pltpu.make_async_remote_copy(
            src_ref=ref_of(level, r, c),
            dst_ref=ref_of(level, r, c),
            send_sem=send_sem.at[0, 0, c],
            recv_sem=recv_sem.at[level, r, c],
            device_id={"seq": dev_x},
            device_id_type=pl.DeviceIdType.MESH,
        ).wait_recv()

    def up_copy(s, c):
        return up_ok & (plane >= s), copy(s, 0, c, 2, s + 1, 0, dev_up, spot)

    def x_copy(s, c):
        return need(s, spot_x, spot, c), copy(s, 0, c, 0, s, 1, dev_x, spot_x)

    def y_copy(s, c):
        return need(s, spot_y, spot, c), copy(s, 0, c, 1, s, 2, dev_y, spot_y)

    def relay_x(s, c):
        cond = need(s, spot_y, spot_x, c) & jnp.logical_not(ends_in_x(s, spot_y, c))
        return cond, copy(s, 1, c, 3, s, 3, dev_y, spot_y)

    def relay_y(s, c):
        return need(s, spot_x, spot_y, c) & ends_in_x(s, spot_x, c), copy(s, 2, c, 4, s, 3, dev_x, spot_x)

    def sends(s, c):
        out = [x_copy(s, c), y_copy(s, c), relay_x(s, c), relay_y(s, c)]
        if s < last_of(c):
            out.append(up_copy(s, c))
        return out

    def q_down(i):
        cols = pl.ds(i * WIDE, WIDE)
        return pltpu.make_async_remote_copy(
            src_ref=q_buf.at[:, cols],
            dst_ref=q_up.at[i],
            send_sem=down_send.at[i],
            recv_sem=down_recv.at[i],
            device_id={"seq": dev_down},
            device_id_type=pl.DeviceIdType.MESH,
        )

    ids_down = pltpu.make_async_remote_copy(
        src_ref=ids_buf.at[0, 0],
        dst_ref=ids_up,
        send_sem=down_send.at[SERVED],
        recv_sem=down_recv.at[SERVED],
        device_id={"seq": dev_down},
        device_id_type=pl.DeviceIdType.MESH,
    )

    def part_up(i):
        return [
            pltpu.make_async_remote_copy(
                src_ref=source.at[i],
                dst_ref=target.at[i],
                send_sem=part_send.at[k, i],
                recv_sem=part_recv.at[k, i],
                device_id={"seq": dev_up},
                device_id_type=pl.DeviceIdType.MESH,
            )
            for k, (source, target) in enumerate(((lse_out, lse_in), (part_out, part_in)))
        ]

    def start(pair):
        pl.when(pair[0])(pair[1].start)

    kv_in = [
        pltpu.make_async_copy(kv_hbm.at[:, :, pl.ds(h * DH, DH)], buf.at[0, h, :, 0], in_sem.at[h]) for h in range(HK)
    ]
    ids_in = pltpu.make_async_copy(ids_hbm, ids_buf.at[0, 0], in_sem.at[HK])
    q_in = pltpu.make_async_copy(q_hbm, q_buf, in_sem.at[HK + 1])
    ids_in.start()
    for one in kv_in:
        one.start()
    q_in.start()

    barrier = pltpu.get_barrier_semaphore()
    for cond, device in ((None, dev_x), (None, dev_y), (up_ok, dev_up), (down_ok, dev_down)):
        def greet(device=device):
            pl.semaphore_signal(barrier, inc=1, device_id={"seq": device}, device_id_type=pl.DeviceIdType.MESH)
        if cond is None:
            greet()
        else:
            pl.when(cond)(greet)
    pl.semaphore_wait(barrier, 2 + up_ok.astype(jnp.int32) + down_ok.astype(jnp.int32))

    def gap_of(level, r):
        return SPAN * (level + later(spots[r], spot)) + spot - spots[r]

    def arrive(s, c):
        if s == 0:
            (ids_in if c == IDS else kv_in[c]).wait()
        else:
            pl.when(plane >= s)(functools.partial(wait_slot, s, 0, c))
        if s < last_of(c):
            start(up_copy(s, c))

    def side(s, c):
        start(x_copy(s, c))
        start(y_copy(s, c))

    def relay(s, c):
        for r, one in ((1, relay_x), (2, relay_y)):
            @pl.when(need(s, spot, spots[r], c))
            def _():
                wait_slot(s - later(spots[r], spot), r, c)
            start(one(s, c))

    def wait_diagonal(level, c):
        pl.when(me >= gap_of(level, 3))(functools.partial(wait_slot, level, 3, c))

    def ask():
        q_in.wait()

        @pl.when(down_ok)
        def _():
            ids_down.start()
            for i in range(SERVED):
                q_down(i).start()

    def clear():
        for level in range(top_level + 1):
            for r in range(SPAN if level < top_level else 1):
                @pl.when(me < gap_of(level, r))
                def _():
                    ids_buf[level, r] = jnp.zeros((1, rows), jnp.int32)

                    def body(h, carry):
                        for k in range(2):
                            buf[level, h, k, r] = jnp.zeros((rows, DH), buf.dtype)
                        return carry

                    lax.fori_loop(0, HK, body, 0)

        @pl.when(jnp.logical_not(down_ok))
        def _():
            for i in range(SERVED):
                lse_in[i] = jnp.full((GROUP, rows), NEG_BIG, jnp.float32)
                part_in[i] = jnp.zeros((rows, WIDE), part_in.dtype)

    row = lax.broadcasted_iota(jnp.int32, (rows, rows), 0)
    col = lax.broadcasted_iota(jnp.int32, (rows, rows), 1)

    def blocks_of(level, top):
        out = [(level, r) for r in range(SPAN)]
        return out + [(level + 1, 0)] if level == top - 1 else out

    def fill(table, query_ids, shift, top):
        own = jnp.broadcast_to(query_ids.astype(jnp.float32), (rows, rows)).T
        for level in range(top):
            for place, (lv, r) in enumerate(blocks_of(level, top)):
                gap = gap_of(lv, r)
                limit = jnp.where(me >= gap, WINDOW, 0)
                distance = (gap + shift) * rows + row - col
                other = jnp.broadcast_to(ids_buf[lv, r].astype(jnp.float32), (rows, rows))
                allowed = (own == other) & (distance >= 0) & (distance < limit)
                table[level, :, place * rows:(place + 1) * rows] = jnp.where(allowed, 0.0, NEG_BIG)

    def make_bias():
        for level in range(top_level):
            wait_diagonal(level, IDS)
        fill(bias, ids_buf[0, 0], 0, top_level)

    def make_bias_up():
        @pl.when(up_ok)
        def _():
            ids_down.wait_recv()
            fill(bias_up, ids_up[...], SPAN, top_level - 1)

    def stack(wide):
        return jnp.concatenate([wide[:, g * DH:(g + 1) * DH] for g in range(GROUP)], axis=0)

    def unstack(tall):
        return jnp.concatenate([tall[g * rows:(g + 1) * rows] for g in range(GROUP)], axis=1)

    def attend(q, c, level, top, table, state):
        blocks = blocks_of(level, top)
        span = len(blocks) * rows

        def side_of(k):
            main = buf[level, c, k].reshape(SPAN * rows, DH)
            if len(blocks) == SPAN:
                return main
            return jnp.concatenate([main, buf[level + 1, c, k, 0]], axis=0)

        t = lax.dot_general(q, side_of(0), (((1,), (1,)), ((), ())), preferred_element_type=jnp.float32)
        t = (t * SCALE2).reshape(GROUP, rows, span) + table[level, :, :span][None]
        t = t.reshape(group_rows, span)
        new = jnp.max(t, axis=1, keepdims=True)
        if state is None:
            new = jnp.broadcast_to(new, (group_rows, DH))
        else:
            new = jnp.maximum(state[0], new)
        p = [jnp.exp2(t[:, r * rows:(r + 1) * rows] - new) for r in range(len(blocks))]
        total = functools.reduce(lambda x, y: x + y, p)
        w = jnp.concatenate([one.astype(jnp.bfloat16) for one in p], axis=1)
        acc = jnp.dot(w, side_of(1), preferred_element_type=jnp.float32)
        if state is not None:
            fix = jnp.exp2(state[0] - new)
            total = total + state[1] * fix
            acc = acc + state[2] * fix
        return new, total, acc

    def keep(c, state):
        run_max[c], run_sum[c], run_acc[c] = state

    def kept(c):
        return run_max[c], run_sum[c], run_acc[c]

    def query(c):
        return stack(q_buf[:, c * WIDE:(c + 1) * WIDE])

    def out_copy(c):
        cols = pl.ds(c * WIDE, WIDE)
        return pltpu.make_async_copy(out_buf.at[:, cols], out_hbm.at[:, cols], out_sem.at[c])

    def finish(c, o):
        out_buf[:, c * WIDE:(c + 1) * WIDE] = unstack(o.astype(out_buf.dtype))
        out_copy(c).start()

    def near(c):
        if c >= SERVED:
            wait_diagonal(0, c)
        keep(c, attend(query(c), c, 0, top_level, bias, None))

    def far(c):
        for level in range(1, top_level):
            wait_diagonal(level, c)
            state = attend(query(c), c, level, top_level, bias, kept(c))
            if level < top_level - 1:
                keep(c, state)
        _, total, acc = state
        finish(c, acc / jnp.sum(total, axis=1, keepdims=True))

    def serve(c):
        for level in range(top_level - 1):
            wait_diagonal(level, c)

        @pl.when(up_ok)
        def _():
            q_down(c).wait_recv()
            state = None
            for level in range(top_level - 1):
                state = attend(stack(q_up[c]), c, level, top_level - 1, bias_up, state)
            most, total, acc = state
            total = jnp.sum(total, axis=1, keepdims=True)
            part_out[c] = unstack((acc / total).astype(part_out.dtype))
            lse = most + jnp.log2(total)
            lse_out[c] = jnp.concatenate(
                [
                    jnp.sum(jnp.where(row == col, lse[g * rows:(g + 1) * rows], 0.0), axis=0, keepdims=True)
                    for g in range(GROUP)
                ],
                axis=0,
            )

    def reply(c):
        @pl.when(up_ok)
        def _():
            for one in part_up(c):
                one.start()

    def merge(c):
        @pl.when(down_ok)
        def _():
            for one in part_up(c):
                one.wait_recv()
        most, total, acc = kept(c)
        total = jnp.sum(total, axis=1, keepdims=True)
        other = jnp.concatenate(
            [
                jnp.sum(jnp.where(row == col, lse_in[c, g:g + 1, :], 0.0), axis=1, keepdims=True)
                for g in range(GROUP)
            ],
            axis=0,
        )
        new = jnp.maximum(most, other)
        fix, weight = jnp.exp2(most - new), jnp.exp2(other - new)
        o = acc * fix + stack(part_in[c]).astype(jnp.float32) * weight
        finish(c, o / (total * fix + weight))

    steps = []

    def add(key, what, *args):
        steps.append((key, len(steps), functools.partial(what, *args)))

    served = [c for c in PIECES if c < SERVED]
    whole = [c for c in PIECES if c >= SERVED and c != IDS]
    order = [IDS] + served + whole
    def came(s, c):
        if s == 0:
            return -5.0
        return 1.5 * s if c == IDS else 4.5 * s + order.index(c) - 3.0

    def relayed(s, c):
        if c == IDS:
            return 1.5 * s + 1.0
        return (4.5 if c < SERVED else 5.5) * s + order.index(c)

    for c in order:
        for s in range(last_of(c) + 1):
            add(came(s, c), arrive, s, c)
            add(came(s, c), side, s, c)
            add(relayed(s, c), relay, s, c)
    add(-4, ask)
    add(-3, clear)
    add(relayed(top_level, IDS) + 0.1, make_bias)
    add(relayed(top_level, IDS) + 0.1, make_bias_up)
    for c in served:
        key = max(relayed(top_level - 1, c) + 2, relayed(top_level, IDS) + 0.2)
        add(key, serve, c)
        add(key + 0.1, near, c)
        add(key + 0.2, reply, c)
        add(key + 9, merge, c)
    for c in whole:
        add(max(relayed(1, c) + 1.5, relayed(top_level, IDS) + 0.2), near, c)
        add(relayed(top_level, c) + 2, far, c)
    for _, _, step in sorted(steps, key=lambda one: one[:2]):
        step()

    for c in order:
        for s in range(last_of(c) + 1):
            for cond, one in sends(s, c):
                pl.when(cond)(one.wait_send)

    @pl.when(down_ok)
    def _():
        ids_down.wait_send()
        for i in range(SERVED):
            q_down(i).wait_send()

    @pl.when(up_ok)
    def _():
        for i in range(SERVED):
            for one in part_up(i):
                one.wait_send()

    for c in range(HK):
        out_copy(c).wait()


def solution(mesh):
    n = mesh.shape["seq"]

    def local(queries, keys_values, segment_ids):
        rows = queries.shape[0]
        reach = min(WINDOW, n * rows // 2)
        back = -(-(reach - 1) // rows)
        assert n % SPAN == 0 and back % SPAN == 0 and back >= 2 * SPAN
        levels = back // SPAN
        group_rows = GROUP * rows
        return pl.pallas_call(
            functools.partial(kernel, n, rows, back),
            out_shape=jax.ShapeDtypeStruct(queries.shape, queries.dtype),
            in_specs=[pl.BlockSpec(memory_space=pl.ANY)] * 3,
            out_specs=pl.BlockSpec(memory_space=pl.ANY),
            scratch_shapes=[
                pltpu.VMEM((levels + 1, HK, 2, SPAN, rows, DH), jnp.bfloat16),
                pltpu.VMEM((levels + 1, SPAN, 1, rows), jnp.int32),
                pltpu.VMEM((rows, HQ * DH), jnp.bfloat16),
                pltpu.VMEM((SERVED, rows, WIDE), jnp.bfloat16),
                pltpu.VMEM((1, rows), jnp.int32),
                pltpu.VMEM((rows, HQ * DH), jnp.bfloat16),
                pltpu.VMEM((SERVED, rows, WIDE), jnp.bfloat16),
                pltpu.VMEM((SERVED, rows, WIDE), jnp.bfloat16),
                pltpu.VMEM((SERVED, GROUP, rows), jnp.float32),
                pltpu.VMEM((SERVED, GROUP, rows), jnp.float32),
                pltpu.VMEM((levels, rows, (SPAN + 1) * rows), jnp.float32),
                pltpu.VMEM((levels - 1, rows, (SPAN + 1) * rows), jnp.float32),
                pltpu.VMEM((HK, group_rows, DH), jnp.float32),
                pltpu.VMEM((HK, group_rows, DH), jnp.float32),
                pltpu.VMEM((HK, group_rows, DH), jnp.float32),
                pltpu.SemaphoreType.DMA((HK + 2,)),
                pltpu.SemaphoreType.DMA((HK,)),
                pltpu.SemaphoreType.DMA((levels + 1, 5, HK + 1)),
                pltpu.SemaphoreType.DMA((levels + 1, SPAN, HK + 1)),
                pltpu.SemaphoreType.DMA((SERVED + 1,)),
                pltpu.SemaphoreType.DMA((SERVED + 1,)),
                pltpu.SemaphoreType.DMA((2, SERVED)),
                pltpu.SemaphoreType.DMA((2, SERVED)),
            ],
            compiler_params=pltpu.CompilerParams(
                collective_id=0, has_side_effects=True, vmem_limit_bytes=60 * 1024 * 1024
            ),
        )(queries, keys_values, segment_ids.reshape(1, rows))

    return jax.shard_map(
        local,
        mesh=mesh,
        in_specs=(P(("rep", "seq"), None), P(None, ("rep", "seq"), None), P(("rep", "seq"))),
        out_specs=P(("rep", "seq"), None),
        check_vma=False,
    )
```

time: 53.9 us -> 56.6 us (1.050)
  the two profiles are of different devices: /device:TPU:28 before, /device:TPU:18 now
where the time goes in v1:
time: 56.6 us; the launch traced here: 56.5 us
  Pallas kernels  54.2 us (96%)
  local copies, waits for them, and re-layouts  2.29 us (4%)
    pallas_call x1, Pallas kernels, local(): pl.pallas_call(functools.partial(kernel, n, rows, back), out_shape=jax.Sh...  54.2 us
    unnamed x1, local copies, waits for them, and re-layouts  2.29 us

profile of v1, /device:TPU:18, one launch (start us, length us, event | category | flops | bytes accessed | tf_op | source)
XLA Modules:
  0.0 56.5 jit_solution(3111710903159793456)
XLA Ops:
  0.0 54.2 %shard_map.37 = bf16[128,4096]{1,0:T(8,128)(2,1)} custom-call(bf16[128,4096]{1,0:T(8,128)(2,1)} %q_hbm.1, bf16[2,128,1024]{2,1,0:T(8,128)(2,1)} %kv_hbm.1, s32[1,128]{1,0:T(1,128)} %bitcast.1), custom_call_target="tpu_custom_call" | custom-call | tf_op jit(solution)/shard_map/pallas_call | solution.py:432
  54.2 2.3 %copy.5 = bf16[128,4096]{1,0:T(8,128)(2,1)} copy(bf16[128,4096]{1,0:T(8,128)(2,1)} %shard_map.37) | data formatting | bytes 2097152

commit v2 on v1

--- a/solution.py
+++ b/solution.py
@@ -22,8 +22,40 @@
 PIECES = [IDS] + list(range(HK))
 
 
-def kernel(n, rows, back, q_hbm, kv_hbm, ids_hbm, out_hbm, buf, ids_buf, q_buf, q_up, ids_up, out_buf, part_out, part_in,
-           lse_out, lse_in, bias, bias_up, run_max, run_sum, run_acc, in_sem, out_sem, send_sem, recv_sem, down_send,
+ORDER = (
+    8, 1, 201, 208, 0, 18, 3, 2, 103, 4, 118, 202, 5, 11, 100, 111, 101, 218, 7, 200, 211, 204, 401, 104, 600, 10,
+    102, 411, 418, 203, 28, 108, 110, 13, 228, 210, 205, 207, 213, 311, 113, 128, 400, 500, 303, 14, 6, 408, 114, 12,
+    428, 206, 112, 301, 15, 214, 212, 402, 308, 410, 106, 105, 404, 318, 403, 17, 117, 300, 314, 217, 215, 24, 25,
+    225, 412, 302, 328, 700, 16, 800, 125, 27, 310, 124, 224, 1000, 312, 313, 1001, 107, 1100, 413, 216, 115, 306,
+    414, 1002, 901, 26, 417, 424, 325, 116, 226, 1102, 305, 425, 900, 405, 127, 1003, 307, 227, 1103, 304, 902, 324,
+    1101, 415, 315, 904, 407, 1200, 426, 406, 903, 316, 416, 1304, 317, 327, 1202, 126, 427, 905, 1305, 1203, 907,
+    906, 1307, 326, 1201, 1306,
+)
+
+
+def plain_order(top_level):
+    keys = {}
+    for c in PIECES:
+        top = top_level - 1 if c < SERVED else top_level
+        for s in range(top + 1):
+            place = s * len(PIECES) + PIECES.index(c)
+            for kind in range(3):
+                keys[kind * 100 + s * 10 + c] = place
+            keys[300 + s * 10 + c] = keys[400 + s * 10 + c] = place + 4
+    end = (top_level + 1) * len(PIECES) + 4
+    for kind in range(5, 9):
+        keys[kind * 100] = end
+    for c in range(HK):
+        for kind in ((10, 9, 11, 12) if c < SERVED else (9, 13)):
+            keys[kind * 100 + c] = end + 1
+    for c in range(SERVED):
+        keys[1200 + c] = end + 2
+        keys[900 + c] = end + 1.5
+    return sorted(keys, key=lambda code: (keys[code], code))
+
+
+def kernel(n, rows, back, q_hbm, kv_hbm, ids_hbm, out_ref, buf, ids_buf, q_buf, q_up, ids_up, part_out, part_in,
+           lse_out, lse_in, bias, bias_up, run_max, run_sum, run_acc, in_sem, send_sem, recv_sem, down_send,
            down_recv, part_send, part_recv):
     top_level = back // SPAN
     planes = n // SPAN
@@ -175,17 +207,6 @@
         if s < last_of(c):
             start(up_copy(s, c))
 
-    def side(s, c):
-        start(x_copy(s, c))
-        start(y_copy(s, c))
-
-    def relay(s, c):
-        for r, one in ((1, relay_x), (2, relay_y)):
-            @pl.when(need(s, spot, spots[r], c))
-            def _():
-                wait_slot(s - later(spots[r], spot), r, c)
-            start(one(s, c))
-
     def wait_diagonal(level, c):
         pl.when(me >= gap_of(level, 3))(functools.partial(wait_slot, level, 3, c))
 
@@ -272,9 +293,10 @@
         else:
             new = jnp.maximum(state[0], new)
         p = [jnp.exp2(t[:, r * rows:(r + 1) * rows] - new) for r in range(len(blocks))]
-        total = functools.reduce(lambda x, y: x + y, p)
         w = jnp.concatenate([one.astype(jnp.bfloat16) for one in p], axis=1)
-        acc = jnp.dot(w, side_of(1), preferred_element_type=jnp.float32)
+        paired = jnp.concatenate([side_of(1), jnp.ones((span, DH), jnp.bfloat16)], axis=1)
+        both = jnp.dot(w, paired, preferred_element_type=jnp.float32)
+        acc, total = both[:, :DH], both[:, DH:]
         if state is not None:
             fix = jnp.exp2(state[0] - new)
             total = total + state[1] * fix
@@ -290,13 +312,8 @@
     def query(c):
         return stack(q_buf[:, c * WIDE:(c + 1) * WIDE])
 
-    def out_copy(c):
-        cols = pl.ds(c * WIDE, WIDE)
-        return pltpu.make_async_copy(out_buf.at[:, cols], out_hbm.at[:, cols], out_sem.at[c])
-
     def finish(c, o):
-        out_buf[:, c * WIDE:(c + 1) * WIDE] = unstack(o.astype(out_buf.dtype))
-        out_copy(c).start()
+        out_ref[:, c * WIDE:(c + 1) * WIDE] = unstack(o.astype(out_ref.dtype))
 
     def near(c):
         if c >= SERVED:
@@ -310,7 +327,7 @@
             if level < top_level - 1:
                 keep(c, state)
         _, total, acc = state
-        finish(c, acc / jnp.sum(total, axis=1, keepdims=True))
+        finish(c, acc / total)
 
     def serve(c):
         for level in range(top_level - 1):
@@ -323,7 +340,6 @@
             for level in range(top_level - 1):
                 state = attend(stack(q_up[c]), c, level, top_level - 1, bias_up, state)
             most, total, acc = state
-            total = jnp.sum(total, axis=1, keepdims=True)
             part_out[c] = unstack((acc / total).astype(part_out.dtype))
             lse = most + jnp.log2(total)
             lse_out[c] = jnp.concatenate(
@@ -346,7 +362,6 @@
             for one in part_up(c):
                 one.wait_recv()
         most, total, acc = kept(c)
-        total = jnp.sum(total, axis=1, keepdims=True)
         other = jnp.concatenate(
             [
                 jnp.sum(jnp.where(row == col, lse_in[c, g:g + 1, :], 0.0), axis=1, keepdims=True)
@@ -359,46 +374,27 @@
         o = acc * fix + stack(part_in[c]).astype(jnp.float32) * weight
         finish(c, o / (total * fix + weight))
 
-    steps = []
-
-    def add(key, what, *args):
-        steps.append((key, len(steps), functools.partial(what, *args)))
-
-    served = [c for c in PIECES if c < SERVED]
-    whole = [c for c in PIECES if c >= SERVED and c != IDS]
-    order = [IDS] + served + whole
-    def came(s, c):
-        if s == 0:
-            return -5.0
-        return 1.5 * s if c == IDS else 4.5 * s + order.index(c) - 3.0
-
-    def relayed(s, c):
-        if c == IDS:
-            return 1.5 * s + 1.0
-        return (4.5 if c < SERVED else 5.5) * s + order.index(c)
-
-    for c in order:
-        for s in range(last_of(c) + 1):
-            add(came(s, c), arrive, s, c)
-            add(came(s, c), side, s, c)
-            add(relayed(s, c), relay, s, c)
-    add(-4, ask)
-    add(-3, clear)
-    add(relayed(top_level, IDS) + 0.1, make_bias)
-    add(relayed(top_level, IDS) + 0.1, make_bias_up)
-    for c in served:
-        key = max(relayed(top_level - 1, c) + 2, relayed(top_level, IDS) + 0.2)
-        add(key, serve, c)
-        add(key + 0.1, near, c)
-        add(key + 0.2, reply, c)
-        add(key + 9, merge, c)
-    for c in whole:
-        add(max(relayed(1, c) + 1.5, relayed(top_level, IDS) + 0.2), near, c)
-        add(relayed(top_level, c) + 2, far, c)
-    for _, _, step in sorted(steps, key=lambda one: one[:2]):
-        step()
-
-    for c in order:
+    def side_x(s, c):
+        start(x_copy(s, c))
+
+    def side_y(s, c):
+        start(y_copy(s, c))
+
+    def relay(r, one, s, c):
+        @pl.when(need(s, spot, spots[r], c))
+        def _():
+            wait_slot(s - later(spots[r], spot), r, c)
+        start(one(s, c))
+
+    actions = (
+        arrive, side_x, side_y, functools.partial(relay, 1, relay_x), functools.partial(relay, 2, relay_y),
+        lambda s, c: ask(), lambda s, c: clear(), lambda s, c: make_bias(), lambda s, c: make_bias_up(),
+        lambda s, c: near(c), lambda s, c: serve(c), lambda s, c: reply(c), lambda s, c: merge(c), lambda s, c: far(c),
+    )
+    for code in ORDER if top_level == 2 else plain_order(top_level):
+        actions[code // 100](code // 10 % 10, code % 10)
+
+    for c in PIECES:
         for s in range(last_of(c) + 1):
             for cond, one in sends(s, c):
                 pl.when(cond)(one.wait_send)
@@ -414,9 +410,6 @@
         for i in range(SERVED):
             for one in part_up(i):
                 one.wait_send()
-
-    for c in range(HK):
-        out_copy(c).wait()
 
 
 def solution(mesh):
@@ -431,16 +424,15 @@
         group_rows = GROUP * rows
         return pl.pallas_call(
             functools.partial(kernel, n, rows, back),
-            out_shape=jax.ShapeDtypeStruct(queries.shape, queries.dtype),
+            out_shape=pltpu.MemorySpace.VMEM(queries.shape, queries.dtype),
             in_specs=[pl.BlockSpec(memory_space=pl.ANY)] * 3,
-            out_specs=pl.BlockSpec(memory_space=pl.ANY),
+            out_specs=pl.BlockSpec(memory_space=pltpu.VMEM),
             scratch_shapes=[
                 pltpu.VMEM((levels + 1, HK, 2, SPAN, rows, DH), jnp.bfloat16),
                 pltpu.VMEM((levels + 1, SPAN, 1, rows), jnp.int32),
                 pltpu.VMEM((rows, HQ * DH), jnp.bfloat16),
                 pltpu.VMEM((SERVED, rows, WIDE), jnp.bfloat16),
                 pltpu.VMEM((1, rows), jnp.int32),
-                pltpu.VMEM((rows, HQ * DH), jnp.bfloat16),
                 pltpu.VMEM((SERVED, rows, WIDE), jnp.bfloat16),
                 pltpu.VMEM((SERVED, rows, WIDE), jnp.bfloat16),
                 pltpu.VMEM((SERVED, GROUP, rows), jnp.float32),
@@ -451,7 +443,6 @@
                 pltpu.VMEM((HK, group_rows, DH), jnp.float32),
                 pltpu.VMEM((HK, group_rows, DH), jnp.float32),
                 pltpu.SemaphoreType.DMA((HK + 2,)),
-                pltpu.SemaphoreType.DMA((HK,)),
                 pltpu.SemaphoreType.DMA((levels + 1, 5, HK + 1)),
                 pltpu.SemaphoreType.DMA((levels + 1, SPAN, HK + 1)),
                 pltpu.SemaphoreType.DMA((SERVED + 1,)),

time: 56.6 us -> 42.3 us (0.75)
  the two profiles are of different devices: /device:TPU:18 before, /device:TPU:28 now
where the time goes in v2:
time: 42.3 us; the launch traced here: 41.8 us
  Pallas kernels  40.8 us (96%)
  local copies, waits for them, and re-layouts  0.97 us (2%)
    pallas_call x1, Pallas kernels, local(): pl.pallas_call(functools.partial(kernel, n, rows, back), out_shape=pltpu....  40.8 us
    unnamed x1, local copies, waits for them, and re-layouts  0.97 us

profile of v2, /device:TPU:28, one launch (start us, length us, event | category | flops | bytes accessed | tf_op | source)
XLA Modules:
  0.0 41.8 jit_solution(16575287178925612239)
XLA Ops:
  0.0 40.8 %shard_map.37 = bf16[128,4096]{1,0:T(8,128)(2,1)S(1)} custom-call(bf16[128,4096]{1,0:T(8,128)(2,1)} %q_hbm.1, bf16[2,128,1024]{2,1,0:T(8,128)(2,1)} %kv_hbm.1, s32[1,128]{1,0:T(1,128)} %bitcast.1), custom_call_target="tpu_custom_call" | custom-call | tf_op jit(solution)/shard_map/pallas_call | solution.py:425
  40.8 1.0 %copy.5 = bf16[128,4096]{1,0:T(8,128)(2,1)} copy(bf16[128,4096]{1,0:T(8,128)(2,1)S(1)} %shard_map.37) | data formatting | bytes 2097152

commit v3 on v2

--- a/solution.py
+++ b/solution.py
@@ -15,36 +15,40 @@
 GROUP = HQ // HK
 WIDE = GROUP * DH
 SPAN = 4
-SERVED = 4
+SERVED = 5
+DETOURED = (6,)
 NEG_BIG = -1e30
 SCALE2 = DH ** (-0.5) * math.log2(math.e)
-IDS = HK
-PIECES = [IDS] + list(range(HK))
+NEAR_IDS, FAR_IDS = HK, HK + 1
+RIDERS = {0: NEAR_IDS, SERVED: FAR_IDS}
 
 
 ORDER = (
-    8, 1, 201, 208, 0, 18, 3, 2, 103, 4, 118, 202, 5, 11, 100, 111, 101, 218, 7, 200, 211, 204, 401, 104, 600, 10,
-    102, 411, 418, 203, 28, 108, 110, 13, 228, 210, 205, 207, 213, 311, 113, 128, 400, 500, 303, 14, 6, 408, 114, 12,
-    428, 206, 112, 301, 15, 214, 212, 402, 308, 410, 106, 105, 404, 318, 403, 17, 117, 300, 314, 217, 215, 24, 25,
-    225, 412, 302, 328, 700, 16, 800, 125, 27, 310, 124, 224, 1000, 312, 313, 1001, 107, 1100, 413, 216, 115, 306,
-    414, 1002, 901, 26, 417, 424, 325, 116, 226, 1102, 305, 425, 900, 405, 127, 1003, 307, 227, 1103, 304, 902, 324,
-    1101, 415, 315, 904, 407, 1200, 426, 406, 903, 316, 416, 1304, 317, 327, 1202, 126, 427, 905, 1305, 1203, 907,
-    906, 1307, 326, 1201, 1306,
+    0, 100, 1, 101, 2, 200, 3, 103, 203, 500, 102, 4, 204, 10, 110, 210, 104, 5, 202, 201, 400, 6, 206, 11, 211, 111,
+    12, 212, 112, 600, 303, 7, 410, 13, 302, 113, 213, 105, 14, 214, 300, 301, 402, 304, 404, 412, 401, 411, 15, 115,
+    215, 114, 311, 403, 310, 700, 800, 107, 406, 16, 216, 1000, 900, 414, 313, 17, 217, 205, 413, 312, 116, 1100,
+    1002, 902, 207, 106, 25, 225, 1001, 1101, 26, 226, 315, 901, 416, 1102, 314, 125, 305, 117, 1004, 1104, 27, 307,
+    227, 1003, 903, 1103, 127, 405, 425, 1200, 126, 1506, 426, 427, 325, 407, 316, 317, 1201, 904, 306, 906, 327,
+    1202, 417, 415, 1400, 905, 1305, 1204, 326, 1306, 907, 1307, 1203,
 )
 
 
 def plain_order(top_level):
     keys = {}
-    for c in PIECES:
+    for c in range(HK):
         top = top_level - 1 if c < SERVED else top_level
         for s in range(top + 1):
-            place = s * len(PIECES) + PIECES.index(c)
+            place = s * HK + c
             for kind in range(3):
                 keys[kind * 100 + s * 10 + c] = place
             keys[300 + s * 10 + c] = keys[400 + s * 10 + c] = place + 4
-    end = (top_level + 1) * len(PIECES) + 4
+    end = (top_level + 1) * HK + 4
+    for c in DETOURED:
+        keys[1500 + c] = HK + c + 8
+        keys[300 + c] = keys[310 + c] = HK + c + 12
     for kind in range(5, 9):
         keys[kind * 100] = end
+    keys[1400] = end
     for c in range(HK):
         for kind in ((10, 9, 11, 12) if c < SERVED else (9, 13)):
             keys[kind * 100 + c] = end + 1
@@ -76,7 +80,22 @@
     dev_down = jnp.where(down_ok, me - SPAN, me + SPAN)
 
     def last_of(c):
-        return top_level - 1 if c < SERVED else top_level
+        return top_level - 1 if c < SERVED or c == NEAR_IDS else top_level
+
+    def carrier(c):
+        return {NEAR_IDS: 0, FAR_IDS: SERVED}.get(c, c)
+
+    def even(c):
+        return carrier(c) % 2 == 0
+
+    def mixed(t):
+        return (t % 2) != (t // 2)
+
+    def by_detour(level, t, c):
+        return mixed(t) & (level == 0) if carrier(c) in DETOURED else t < 0
+
+    def load(c):
+        return [RIDERS[c], c] if c in RIDERS else [c]
 
     def later(block, t):
         return (block > t).astype(jnp.int32)
@@ -86,15 +105,14 @@
         return (plane >= s) & (gap >= 1) & (gap <= SPAN * last_of(c))
 
     def ends_in_x(s, t, c):
-        mixed = (t % 2) != (t // 2)
         edge = s == 0 or s == last_of(c)
         if edge:
-            return mixed | (c % 2 == 0)
-        return jnp.logical_not(mixed) & (c % 2 == 0)
+            return mixed(t) | even(c)
+        return jnp.logical_not(mixed(t)) & even(c)
 
     def ref_of(level, r, c):
-        if c == IDS:
-            return ids_buf.at[level, r]
+        if c >= HK:
+            return ids_buf.at[c - HK, level, r]
         return buf.at[level, c, :, r]
 
     def copy(s, r, c, lane, to_s, to_r, device, to_spot):
@@ -118,11 +136,15 @@
             device_id_type=pl.DeviceIdType.MESH,
         ).wait_recv()
 
+    def gap_of(level, r):
+        return SPAN * (level + later(spots[r], spot)) + spot - spots[r]
+
     def up_copy(s, c):
         return up_ok & (plane >= s), copy(s, 0, c, 2, s + 1, 0, dev_up, spot)
 
     def x_copy(s, c):
-        return need(s, spot_x, spot, c), copy(s, 0, c, 0, s, 1, dev_x, spot_x)
+        direct = jnp.logical_not(by_detour(s - later(spot, spot_x), spot_x, c))
+        return need(s, spot_x, spot, c) & direct, copy(s, 0, c, 0, s, 1, dev_x, spot_x)
 
     def y_copy(s, c):
         return need(s, spot_y, spot, c), copy(s, 0, c, 1, s, 2, dev_y, spot_y)
@@ -134,8 +156,21 @@
     def relay_y(s, c):
         return need(s, spot_x, spot_y, c) & ends_in_x(s, spot_x, c), copy(s, 2, c, 4, s, 3, dev_x, spot_x)
 
+    def detour(c):
+        s = later(spot_d, spot)
+        cond = (me >= gap_of(0, 3)) & need(s, spot_y, spot_d, c) & by_detour(s - later(spot_d, spot_y), spot_y, c)
+        return cond, pltpu.make_async_remote_copy(
+            src_ref=ref_of(0, 3, c),
+            dst_ref=ref_of(s - later(spot_d, spot_y), 1, c),
+            send_sem=send_sem.at[0, 5, c],
+            recv_sem=recv_sem.at[s - later(spot_d, spot_y), 1, c],
+            device_id={"seq": dev_y},
+            device_id_type=pl.DeviceIdType.MESH,
+        )
+
     def sends(s, c):
-        out = [x_copy(s, c), y_copy(s, c), relay_x(s, c), relay_y(s, c)]
+        out = [detour(c)] if s == 0 and carrier(c) in DETOURED else []
+        out += [x_copy(s, c), y_copy(s, c), relay_x(s, c), relay_y(s, c)]
         if s < last_of(c):
             out.append(up_copy(s, c))
         return out
@@ -152,7 +187,7 @@
         )
 
     ids_down = pltpu.make_async_remote_copy(
-        src_ref=ids_buf.at[0, 0],
+        src_ref=ids_buf.at[0, 0, 0],
         dst_ref=ids_up,
         send_sem=down_send.at[SERVED],
         recv_sem=down_recv.at[SERVED],
@@ -179,9 +214,10 @@
     kv_in = [
         pltpu.make_async_copy(kv_hbm.at[:, :, pl.ds(h * DH, DH)], buf.at[0, h, :, 0], in_sem.at[h]) for h in range(HK)
     ]
-    ids_in = pltpu.make_async_copy(ids_hbm, ids_buf.at[0, 0], in_sem.at[HK])
-    q_in = pltpu.make_async_copy(q_hbm, q_buf, in_sem.at[HK + 1])
-    ids_in.start()
+    ids_in = [pltpu.make_async_copy(ids_hbm, ids_buf.at[k, 0, 0], in_sem.at[HK + k]) for k in range(2)]
+    q_in = pltpu.make_async_copy(q_hbm, q_buf, in_sem.at[HK + 2])
+    for one in ids_in:
+        one.start()
     for one in kv_in:
         one.start()
     q_in.start()
@@ -196,16 +232,19 @@
             pl.when(cond)(greet)
     pl.semaphore_wait(barrier, 2 + up_ok.astype(jnp.int32) + down_ok.astype(jnp.int32))
 
-    def gap_of(level, r):
-        return SPAN * (level + later(spots[r], spot)) + spot - spots[r]
-
     def arrive(s, c):
-        if s == 0:
-            (ids_in if c == IDS else kv_in[c]).wait()
-        else:
-            pl.when(plane >= s)(functools.partial(wait_slot, s, 0, c))
-        if s < last_of(c):
-            start(up_copy(s, c))
+        for k in load(c):
+            if s == 0:
+                (ids_in[k - HK] if k >= HK else kv_in[k]).wait()
+            else:
+                pl.when(plane >= s)(functools.partial(wait_slot, s, 0, k))
+            if s < last_of(k):
+                start(up_copy(s, k))
+
+    def pass_on(c):
+        for k in load(c):
+            wait_diagonal(0, k)
+            start(detour(k))
 
     def wait_diagonal(level, c):
         pl.when(me >= gap_of(level, 3))(functools.partial(wait_slot, level, 3, c))
@@ -224,7 +263,8 @@
             for r in range(SPAN if level < top_level else 1):
                 @pl.when(me < gap_of(level, r))
                 def _():
-                    ids_buf[level, r] = jnp.zeros((1, rows), jnp.int32)
+                    for k in range(2):
+                        ids_buf[k, level, r] = jnp.zeros((1, rows), jnp.int32)
 
                     def body(h, carry):
                         for k in range(2):
@@ -246,27 +286,32 @@
         out = [(level, r) for r in range(SPAN)]
         return out + [(level + 1, 0)] if level == top - 1 else out
 
-    def fill(table, query_ids, shift, top):
+    def fill(table, known, query_ids, shift, begin, end, top):
         own = jnp.broadcast_to(query_ids.astype(jnp.float32), (rows, rows)).T
-        for level in range(top):
+        for level in range(begin, end):
             for place, (lv, r) in enumerate(blocks_of(level, top)):
                 gap = gap_of(lv, r)
                 limit = jnp.where(me >= gap, WINDOW, 0)
                 distance = (gap + shift) * rows + row - col
-                other = jnp.broadcast_to(ids_buf[lv, r].astype(jnp.float32), (rows, rows))
+                other = jnp.broadcast_to(ids_buf[known, lv, r].astype(jnp.float32), (rows, rows))
                 allowed = (own == other) & (distance >= 0) & (distance < limit)
                 table[level, :, place * rows:(place + 1) * rows] = jnp.where(allowed, 0.0, NEG_BIG)
 
     def make_bias():
-        for level in range(top_level):
-            wait_diagonal(level, IDS)
-        fill(bias, ids_buf[0, 0], 0, top_level)
+        for level in range(top_level - 1):
+            wait_diagonal(level, NEAR_IDS)
+        fill(bias, 0, ids_buf[0, 0, 0], 0, 0, 1, top_level)
+
+    def make_bias_far():
+        for level in range(SERVED in DETOURED, top_level):
+            wait_diagonal(level, FAR_IDS)
+        fill(bias, 1, ids_buf[0, 0, 0], 0, 1, top_level, top_level)
 
     def make_bias_up():
         @pl.when(up_ok)
         def _():
             ids_down.wait_recv()
-            fill(bias_up, ids_up[...], SPAN, top_level - 1)
+            fill(bias_up, 0, ids_up[...], SPAN, 0, top_level - 1, top_level - 1)
 
     def stack(wide):
         return jnp.concatenate([wide[:, g * DH:(g + 1) * DH] for g in range(GROUP)], axis=0)
@@ -316,7 +361,7 @@
         out_ref[:, c * WIDE:(c + 1) * WIDE] = unstack(o.astype(out_ref.dtype))
 
     def near(c):
-        if c >= SERVED:
+        if c >= SERVED and c not in DETOURED:
             wait_diagonal(0, c)
         keep(c, attend(query(c), c, 0, top_level, bias, None))
 
@@ -375,41 +420,49 @@
         finish(c, o / (total * fix + weight))
 
     def side_x(s, c):
-        start(x_copy(s, c))
+        for k in load(c):
+            start(x_copy(s, k))
 
     def side_y(s, c):
-        start(y_copy(s, c))
+        for k in load(c):
+            start(y_copy(s, k))
 
     def relay(r, one, s, c):
-        @pl.when(need(s, spot, spots[r], c))
-        def _():
-            wait_slot(s - later(spots[r], spot), r, c)
-        start(one(s, c))
+        for k in load(c):
+            @pl.when(need(s, spot, spots[r], k))
+            def _():
+                wait_slot(s - later(spots[r], spot), r, k)
+            start(one(s, k))
 
     actions = (
         arrive, side_x, side_y, functools.partial(relay, 1, relay_x), functools.partial(relay, 2, relay_y),
         lambda s, c: ask(), lambda s, c: clear(), lambda s, c: make_bias(), lambda s, c: make_bias_up(),
         lambda s, c: near(c), lambda s, c: serve(c), lambda s, c: reply(c), lambda s, c: merge(c), lambda s, c: far(c),
+        lambda s, c: make_bias_far(), lambda s, c: pass_on(c),
     )
-    for code in ORDER if top_level == 2 else plain_order(top_level):
+    def settle():
+        for c in range(HK + 2):
+            for s in range(last_of(c) + 1):
+                for cond, one in sends(s, c):
+                    pl.when(cond)(one.wait_send)
+
+        @pl.when(down_ok)
+        def _():
+            ids_down.wait_send()
+            for i in range(SERVED):
+                q_down(i).wait_send()
+
+        @pl.when(up_ok)
+        def _():
+            for i in range(SERVED):
+                for one in part_up(i):
+                    one.wait_send()
+
+    order = ORDER if top_level == 2 else plain_order(top_level)
+    for place, code in enumerate(order):
+        if place == len(order) - 1:
+            settle()
         actions[code // 100](code // 10 % 10, code % 10)
-
-    for c in PIECES:
-        for s in range(last_of(c) + 1):
-            for cond, one in sends(s, c):
-                pl.when(cond)(one.wait_send)
-
-    @pl.when(down_ok)
-    def _():
-        ids_down.wait_send()
-        for i in range(SERVED):
-            q_down(i).wait_send()
-
-    @pl.when(up_ok)
-    def _():
-        for i in range(SERVED):
-            for one in part_up(i):
-                one.wait_send()
 
 
 def solution(mesh):
@@ -429,7 +482,7 @@
             out_specs=pl.BlockSpec(memory_space=pltpu.VMEM),
             scratch_shapes=[
                 pltpu.VMEM((levels + 1, HK, 2, SPAN, rows, DH), jnp.bfloat16),
-                pltpu.VMEM((levels + 1, SPAN, 1, rows), jnp.int32),
+                pltpu.VMEM((2, levels + 1, SPAN, 1, rows), jnp.int32),
                 pltpu.VMEM((rows, HQ * DH), jnp.bfloat16),
                 pltpu.VMEM((SERVED, rows, WIDE), jnp.bfloat16),
                 pltpu.VMEM((1, rows), jnp.int32),
@@ -442,9 +495,9 @@
                 pltpu.VMEM((HK, group_rows, DH), jnp.float32),
                 pltpu.VMEM((HK, group_rows, DH), jnp.float32),
                 pltpu.VMEM((HK, group_rows, DH), jnp.float32),
-                pltpu.SemaphoreType.DMA((HK + 2,)),
-                pltpu.SemaphoreType.DMA((levels + 1, 5, HK + 1)),
-                pltpu.SemaphoreType.DMA((levels + 1, SPAN, HK + 1)),
+                pltpu.SemaphoreType.DMA((HK + 3,)),
+                pltpu.SemaphoreType.DMA((levels + 1, 6, HK + 2)),
+                pltpu.SemaphoreType.DMA((levels + 1, SPAN, HK + 2)),
                 pltpu.SemaphoreType.DMA((SERVED + 1,)),
                 pltpu.SemaphoreType.DMA((SERVED + 1,)),
                 pltpu.SemaphoreType.DMA((2, SERVED)),

time: 42.3 us -> 39.3 us (0.929)
  Pallas kernels: 40.8 us -> 38.2 us
    pallas_call x1, Pallas kernels: 40.8 us -> 38.2 us  [local(): pl.pallas_call(functools.partial(kernel, n, rows, back), out_shape=pltpu....]
where the time goes in v3:
time: 39.3 us; the launch traced here: 39.2 us
  Pallas kernels  38.2 us (97%)
  local copies, waits for them, and re-layouts  0.97 us (2%)
    pallas_call x1, Pallas kernels, local(): pl.pallas_call(functools.partial(kernel, n, rows, back), out_shape=pltpu....  38.2 us
    unnamed x1, local copies, waits for them, and re-layouts  0.97 us

profile of v3, /device:TPU:28, one launch (start us, length us, event | category | flops | bytes accessed | tf_op | source)
XLA Modules:
  0.0 39.2 jit_solution(16197310425602470513)
XLA Ops:
  0.0 38.2 %shard_map.37 = bf16[128,4096]{1,0:T(8,128)(2,1)S(1)} custom-call(bf16[128,4096]{1,0:T(8,128)(2,1)} %q_hbm.1, bf16[2,128,1024]{2,1,0:T(8,128)(2,1)} %kv_hbm.1, s32[1,128]{1,0:T(1,128)} %bitcast.1), custom_call_target="tpu_custom_call" | custom-call | tf_op jit(solution)/shard_map/pallas_call | solution.py:478
  38.2 1.0 %copy.5 = bf16[128,4096]{1,0:T(8,128)(2,1)} copy(bf16[128,4096]{1,0:T(8,128)(2,1)S(1)} %shard_map.37) | data formatting | bytes 2097152

commit v4 on v3

--- a/solution.py
+++ b/solution.py
@@ -17,6 +17,7 @@
 SPAN = 4
 SERVED = 5
 DETOURED = (6,)
+ENDS_X = (0, 2, 6, 7)
 NEG_BIG = -1e30
 SCALE2 = DH ** (-0.5) * math.log2(math.e)
 NEAR_IDS, FAR_IDS = HK, HK + 1
@@ -24,12 +25,12 @@
 
 
 ORDER = (
-    0, 100, 1, 101, 2, 200, 3, 103, 203, 500, 102, 4, 204, 10, 110, 210, 104, 5, 202, 201, 400, 6, 206, 11, 211, 111,
-    12, 212, 112, 600, 303, 7, 410, 13, 302, 113, 213, 105, 14, 214, 300, 301, 402, 304, 404, 412, 401, 411, 15, 115,
-    215, 114, 311, 403, 310, 700, 800, 107, 406, 16, 216, 1000, 900, 414, 313, 17, 217, 205, 413, 312, 116, 1100,
-    1002, 902, 207, 106, 25, 225, 1001, 1101, 26, 226, 315, 901, 416, 1102, 314, 125, 305, 117, 1004, 1104, 27, 307,
-    227, 1003, 903, 1103, 127, 405, 425, 1200, 126, 1506, 426, 427, 325, 407, 316, 317, 1201, 904, 306, 906, 327,
-    1202, 417, 415, 1400, 905, 1305, 1204, 326, 1306, 907, 1307, 1203,
+    0, 200, 1, 101, 500, 2, 202, 102, 100, 4, 104, 6, 10, 110, 210, 206, 201, 204, 106, 11, 111, 211, 400, 5, 105, 12,
+    112, 212, 410, 14, 114, 205, 214, 3, 7, 411, 301, 103, 311, 16, 300, 216, 412, 401, 15, 215, 402, 116, 203, 406,
+    107, 600, 310, 700, 13, 113, 304, 414, 404, 312, 213, 800, 1000, 17, 217, 314, 302, 1001, 26, 226, 1100, 416,
+    1101, 207, 900, 901, 115, 25, 225, 1002, 902, 415, 27, 125, 403, 305, 117, 405, 313, 316, 126, 1102, 227, 127,
+    303, 307, 413, 1506, 315, 1004, 1104, 325, 1200, 425, 904, 426, 417, 306, 906, 1201, 407, 1003, 903, 427, 317,
+    1202, 905, 1103, 1400, 1305, 326, 1306, 1204, 327, 907, 1307, 1203,
 )
 
 
@@ -85,8 +86,8 @@
     def carrier(c):
         return {NEAR_IDS: 0, FAR_IDS: SERVED}.get(c, c)
 
-    def even(c):
-        return carrier(c) % 2 == 0
+    def chosen(c):
+        return carrier(c) in ENDS_X
 
     def mixed(t):
         return (t % 2) != (t // 2)
@@ -107,13 +108,13 @@
     def ends_in_x(s, t, c):
         edge = s == 0 or s == last_of(c)
         if edge:
-            return mixed(t) | even(c)
-        return jnp.logical_not(mixed(t)) & even(c)
+            return mixed(t) | chosen(c)
+        return jnp.logical_not(mixed(t)) & chosen(c)
 
     def ref_of(level, r, c):
         if c >= HK:
             return ids_buf.at[c - HK, level, r]
-        return buf.at[level, c, :, r]
+        return buf.at[level, c, r]
 
     def copy(s, r, c, lane, to_s, to_r, device, to_spot):
         level, to_level = s - later(spots[r], spot), to_s - later(spots[r], to_spot)
@@ -212,7 +213,7 @@
         pl.when(pair[0])(pair[1].start)
 
     kv_in = [
-        pltpu.make_async_copy(kv_hbm.at[:, :, pl.ds(h * DH, DH)], buf.at[0, h, :, 0], in_sem.at[h]) for h in range(HK)
+        pltpu.make_async_copy(kv_hbm.at[:, :, pl.ds(h * DH, DH)], buf.at[0, h, 0], in_sem.at[h]) for h in range(HK)
     ]
     ids_in = [pltpu.make_async_copy(ids_hbm, ids_buf.at[k, 0, 0], in_sem.at[HK + k]) for k in range(2)]
     q_in = pltpu.make_async_copy(q_hbm, q_buf, in_sem.at[HK + 2])
@@ -268,7 +269,7 @@
 
                     def body(h, carry):
                         for k in range(2):
-                            buf[level, h, k, r] = jnp.zeros((rows, DH), buf.dtype)
+                            buf[level, h, r, k] = jnp.zeros((rows, DH), buf.dtype)
                         return carry
 
                     lax.fori_loop(0, HK, body, 0)
@@ -324,10 +325,10 @@
         span = len(blocks) * rows
 
         def side_of(k):
-            main = buf[level, c, k].reshape(SPAN * rows, DH)
+            main = buf[level, c, :, k].reshape(SPAN * rows, DH)
             if len(blocks) == SPAN:
                 return main
-            return jnp.concatenate([main, buf[level + 1, c, k, 0]], axis=0)
+            return jnp.concatenate([main, buf[level + 1, c, 0, k]], axis=0)
 
         t = lax.dot_general(q, side_of(0), (((1,), (1,)), ((), ())), preferred_element_type=jnp.float32)
         t = (t * SCALE2).reshape(GROUP, rows, span) + table[level, :, :span][None]
@@ -481,7 +482,7 @@
             in_specs=[pl.BlockSpec(memory_space=pl.ANY)] * 3,
             out_specs=pl.BlockSpec(memory_space=pltpu.VMEM),
             scratch_shapes=[
-                pltpu.VMEM((levels + 1, HK, 2, SPAN, rows, DH), jnp.bfloat16),
+                pltpu.VMEM((levels + 1, HK, SPAN, 2, rows, DH), jnp.bfloat16),
                 pltpu.VMEM((2, levels + 1, SPAN, 1, rows), jnp.int32),
                 pltpu.VMEM((rows, HQ * DH), jnp.bfloat16),
                 pltpu.VMEM((SERVED, rows, WIDE), jnp.bfloat16),

time: 39.3 us -> 38.9 us (0.990)
  Pallas kernels: 38.2 us -> 37.6 us
    pallas_call x1, Pallas kernels: 38.2 us -> 37.6 us  [local(): pl.pallas_call(functools.partial(kernel, n, rows, back), out_shape=pltpu....]
where the time goes in v4:
time: 38.9 us; the launch traced here: 38.6 us
  Pallas kernels  37.6 us (97%)
  local copies, waits for them, and re-layouts  0.97 us (2%)
    pallas_call x1, Pallas kernels, local(): pl.pallas_call(functools.partial(kernel, n, rows, back), out_shape=pltpu....  37.6 us
    unnamed x1, local copies, waits for them, and re-layouts  0.97 us

profile of v4, /device:TPU:28, one launch (start us, length us, event | category | flops | bytes accessed | tf_op | source)
XLA Modules:
  0.0 38.6 jit_solution(11436092880813418091)
XLA Ops:
  0.0 37.6 %shard_map.37 = bf16[128,4096]{1,0:T(8,128)(2,1)S(1)} custom-call(bf16[128,4096]{1,0:T(8,128)(2,1)} %q_hbm.1, bf16[2,128,1024]{2,1,0:T(8,128)(2,1)} %kv_hbm.1, s32[1,128]{1,0:T(1,128)} %bitcast.1), custom_call_target="tpu_custom_call" | custom-call | tf_op jit(solution)/shard_map/pallas_call | solution.py:479
  37.6 1.0 %copy.5 = bf16[128,4096]{1,0:T(8,128)(2,1)} copy(bf16[128,4096]{1,0:T(8,128)(2,1)S(1)} %shard_map.37) | data formatting | bytes 2097152

commit v5 on v4

--- a/solution.py
+++ b/solution.py
@@ -140,8 +140,13 @@
     def gap_of(level, r):
         return SPAN * (level + later(spots[r], spot)) + spot - spots[r]
 
+    def arrives(s, at, c):
+        if c < SERVED and s == last_of(c):
+            return (at >= s) & ((at < planes - 1) | (spot > 0))
+        return at >= s
+
     def up_copy(s, c):
-        return up_ok & (plane >= s), copy(s, 0, c, 2, s + 1, 0, dev_up, spot)
+        return up_ok & (plane >= s) & arrives(s + 1, plane + 1, c), copy(s, 0, c, 2, s + 1, 0, dev_up, spot)
 
     def x_copy(s, c):
         direct = jnp.logical_not(by_detour(s - later(spot, spot_x), spot_x, c))
@@ -238,7 +243,7 @@
             if s == 0:
                 (ids_in[k - HK] if k >= HK else kv_in[k]).wait()
             else:
-                pl.when(plane >= s)(functools.partial(wait_slot, s, 0, k))
+                pl.when(arrives(s, plane, k))(functools.partial(wait_slot, s, 0, k))
             if s < last_of(k):
                 start(up_copy(s, k))
 

time: 38.9 us -> 38.9 us (level)
  no operation moved by 1% of the time
where the time goes in v5:
time: 38.9 us; the launch traced here: 38.6 us
  Pallas kernels  37.6 us (97%)
  local copies, waits for them, and re-layouts  0.97 us (2%)
    pallas_call x1, Pallas kernels, local(): pl.pallas_call(functools.partial(kernel, n, rows, back), out_shape=pltpu....  37.6 us
    unnamed x1, local copies, waits for them, and re-layouts  0.97 us

profile of v5, /device:TPU:28, one launch (start us, length us, event | category | flops | bytes accessed | tf_op | source)
XLA Modules:
  0.0 38.6 jit_solution(17018459952130847505)
XLA Ops:
  0.0 37.6 %shard_map.37 = bf16[128,4096]{1,0:T(8,128)(2,1)S(1)} custom-call(bf16[128,4096]{1,0:T(8,128)(2,1)} %q_hbm.1, bf16[2,128,1024]{2,1,0:T(8,128)(2,1)} %kv_hbm.1, s32[1,128]{1,0:T(1,128)} %bitcast.1), custom_call_target="tpu_custom_call" | custom-call | tf_op jit(solution)/shard_map/pallas_call | solution.py:484
  37.6 1.0 %copy.5 = bf16[128,4096]{1,0:T(8,128)(2,1)} copy(bf16[128,4096]{1,0:T(8,128)(2,1)S(1)} %shard_map.37) | data formatting | bytes 2097152
